TPU v7x, 256 devices: a whole 4x4x8 slice. The times are simulated.
256 devices in a mesh: grp: 16 (over x_lo, y, core), sp: 16 (over z, x_hi).
Axes of the slice: x: 4 (x_hi: 2, x_lo: 2; x = x_hi * 2 + x_lo), y: 4, z: 8, core: 2. Of those that a mesh axis runs over, the one named last changes fastest.
Arguments:
- latents: bfloat16 [16, 2048, 3072], P('grp', 'sp'), may hold values from -6 to 6
- timestep: int32 [16], P('grp'), may hold values from 0 to 999
- w_mod: bfloat16 [256, 9216], replicated, may hold values from -0.375 to 0.375
- w_qkv: bfloat16 [16, 3072, 384], P('sp', 'grp'), may hold values from -2 to 2
- w_out: bfloat16 [16, 128, 3072], P('sp', 'grp'), may hold values from -0.5 to 0.5
Outputs:
- update: bfloat16 [16, 2048, 3072], P('grp', 'sp')
All inputs are finite; a program needn't handle non-finite values.
Results may differ from a plain program's by a relative error of at most 0.012.
Values may be sent and summed in bfloat16 or wider, within the bound.
A program may use at most 128 MiB of HBM per device.

v0:
```python
import math

import jax
import jax.numpy as jnp
from jax import lax
from jax.sharding import PartitionSpec as P


def sent_to_all(x, axis):
    copies = jnp.broadcast_to(x, (lax.axis_size(axis), *x.shape))
    return lax.all_to_all(copies, axis, split_axis=0, concat_axis=0, tiled=True)


def laid_out(tiles, dim):
    shape = list(tiles.shape[1:])
    shape[dim] *= tiles.shape[0]
    return jnp.moveaxis(tiles, 0, dim).reshape(shape)


def gathered_copies(x, axis, dim):
    tiles = sent_to_all(x, axis)
    return laid_out(tiles, dim)


def modulation(timestep, w_mod):
    half_freq = w_mod.shape[0] // 2
    freqs = jnp.exp(-math.log(10000.0) * jnp.arange(half_freq, dtype=jnp.float32) / half_freq)
    angles = timestep.astype(jnp.float32)[:, None] * freqs[None, :]
    embed = jnp.concatenate([jnp.cos(angles), jnp.sin(angles)], axis=1).astype(jnp.bfloat16)
    return jnp.dot(embed, w_mod, preferred_element_type=jnp.float32)


def normalize(latents, shift, scale):
    values = latents.astype(jnp.float32)
    center = jnp.mean(values, axis=-1, keepdims=True)
    spread = jnp.mean((values - center) ** 2, axis=-1, keepdims=True)
    normed = (values - center) * lax.rsqrt(spread + 1e-06)
    return (normed * (1.0 + scale[:, None, :]) + shift[:, None, :]).astype(jnp.bfloat16)


def attend(query, keys, values):
    length, head_size = query.shape
    block = min(512, length)
    blocks = query.reshape(length // block, block, head_size)

    def one_block(query_rows):
        scores = lax.dot_general(
            query_rows, keys, (((1,), (1,)), ((), ())), preferred_element_type=jnp.float32
        )
        scores = scores / math.sqrt(head_size)
        largest = jnp.max(scores, axis=1, keepdims=True)
        weights = jnp.exp(scores - largest)
        probs = (weights / jnp.sum(weights, axis=1, keepdims=True)).astype(jnp.bfloat16)
        return jnp.dot(probs, values, preferred_element_type=jnp.float32).astype(jnp.bfloat16)

    return lax.map(one_block, blocks).reshape(length, head_size)


def on_device(latents, timestep, w_mod, w_qkv, w_out):
    images, tok_local, width = latents.shape
    triple = w_qkv.shape[2]
    head_size = triple // 3
    mod = modulation(timestep, w_mod)
    shift = mod[:, :width]
    scale = mod[:, width : 2 * width]
    gate = mod[:, 2 * width :]
    normed = normalize(latents, shift, scale)
    whole = lax.all_gather(normed, "sp", axis=1, tiled=True)
    qkv_sum = jnp.einsum(
        "itc,cf->itf",
        whole,
        gathered_copies(w_qkv, "grp", 1)[0],
        preferred_element_type=jnp.float32,
    )
    qkv = qkv_sum.astype(jnp.bfloat16)
    out_rows = gathered_copies(w_out, "grp", 1)
    every_head = lax.all_gather(out_rows, "sp", axis=0, tiled=True)
    attended = jnp.stack(
        [
            attend(
                qkv[0, :, :head_size],
                qkv[0, :, head_size : 2 * head_size],
                qkv[0, :, 2 * head_size :],
            )
        ]
    )
    mine = lax.all_to_all(attended, "sp", split_axis=1, concat_axis=2, tiled=True)
    count = every_head.shape[0]
    mixed = mine.reshape(images, tok_local, count, head_size)
    contrib = jnp.einsum(
        "itnc,ncd->itnd", mixed, every_head, preferred_element_type=jnp.float32
    ).astype(jnp.bfloat16)
    contrib = lax.optimization_barrier(contrib)
    total = jnp.sum(contrib.astype(jnp.float32), axis=2)
    return (gate[:, None, :] * total).astype(jnp.bfloat16)


def solution(mesh):
    placed = (P("grp", "sp", None), P("grp"), P(), P("sp", "grp", None), P("sp", "grp", None))
    return jax.shard_map(
        on_device, mesh=mesh, in_specs=placed, out_specs=P("grp", "sp", None), check_vma=False
    )
```

profile of v0, /device:TPU:1, one launch (start us, length us, event | category | flops | bytes accessed | tf_op | source)
XLA Modules:
  0.0 408.2 jit_solution(1425619867085390423)
XLA Ops:
  7.4 3.1 fusion.26
  10.7 0.4 fusion.20
  11.0 1.3 fusion.23
  12.5 19.6 %all_to_all.25 = bf16[16,1,8,3072]{3,2,1,0:T(8,128)(2,1)} all-to-all(bf16[16,1,8,3072]{3,2,1,0:T(8,128)(2,1)S(1)} %broadcast_in_dim.11), channel_id=1, replica_groups=mesh['grp'=16,'sp'=16] {'grp'}, dimensions={0} | all-to-all | bytes 1572864 | tf_op jit(solution)/shard_map/all_to_all | solution.py:11
  32.1 1.8 broadcast_in_dim.10
  33.9 4.4 %all-to-all-start = ((bf16[16,1,192,384]{3,2,1,0:T(8,128)(2,1)}), bf16[16,1,192,384]{3,2,1,0:T(8,128)(2,1)S(1)}, u32[]{:S(2)}, u32[]{:S(2)}) async-start(bf16[16,1,192,384]{3,2,1,0:T(8,128)(2,1)} %broadcast_in_dim.10), calls=%async_computation | async-start | bytes 4718592 | tf_op jit(solution)/shard_map/all_to_all | solution.py:11
  38.3 30.7 %all-to-all-done = bf16[16,1,192,384]{3,2,1,0:T(8,128)(2,1)S(1)} async-done(((bf16[16,1,192,384]{3,2,1,0:T(8,128)(2,1)}), bf16[16,1,192,384]{3,2,1,0:T(8,128)(2,1)S(1)}, u32[]{:S(2)}, u32[]{:S(2)}) %all-to-all-start) | async-done | bytes 2359328 | tf_op jit(solution)/shard_map/all_to_all | solution.py:11
  69.0 124.8 %all-gather.3.cloned.1.call-done = bf16[1,2048,3072]{2,1,0:T(8,128)(2,1)} async-done(((bf16[1,128,3072]{2,1,0:T(8,128)(2,1)}), bf16[1,2048,3072]{2,1,0:T(8,128)(2,1)}) %all-gather.3.cloned.1.call-update) | async-done | bytes 12582928 | tf_op jit(solution)/shard_map/all_gather | solution.py:68
  193.9 9.6 %fusion.15 = bf16[1,2048,384]{2,1,0:T(8,128)(2,1)S(1)} fusion(bf16[3072,384]{1,0:T(8,128)(2,1)S(1)} %bitcast.72, bf16[1,2048,3072]{2,1,0:T(8,128)(2,1)} %all-gather.3.cloned.1.call-done), kind=kOutput, calls=%fused_computation.18 | convolution fusion | flops 4832624640 | bytes 16515072 | tf_op jit(solution)/shard_map/itc,cf->itf/dot_general | solution.py:69
  203.5 0.3 slice_bitcast_fusion
  203.8 10.6 %while.10 = (s32[]{:T(128)}, bf16[4,512,128]{2,1,0:T(8,128)(2,1)S(1)}, bf16[4,512,128]{2,1,0:T(8,128)(2,1)S(1)}, bf16[2048,128]{1,0:T(8,128)(2,1)S(1)}, bf16[2048,128]{1,0:T(8,128)(2,1)S(1)}, /*index=5*/s32[]{:T(128)}) while((s32[]{:T(128)}, bf16[4,512,128]{2,1,0:T(8,128)(2,1)S(1)}, bf16[4,512,128]{2,1,0:T(8,128)(2,1)S(1)}, ...), condition=%wide.region_5.6_spmd, body=%wide.region_2.5_spmd.sunk | while | flops 546372608 | bytes 13903949 | solution.py:56
  203.8 0.8 multiply_reduce_fusion.2
  204.6 0.8 fusion.40
  205.4 1.0 fusion.41
  206.5 0.8 multiply_reduce_fusion.2
  207.2 0.8 fusion.40
  208.1 1.0 fusion.41
  209.1 0.8 multiply_reduce_fusion.2
  209.9 0.8 fusion.40
  210.7 1.0 fusion.41
  211.8 0.8 multiply_reduce_fusion.2
  212.6 0.8 fusion.40
  213.4 1.0 fusion.41
  214.4 8.1 %copy.9 = bf16[1,2048,128]{2,0,1:T(2,128)(2,1)S(1)} copy(bf16[1,2048,128]{2,1,0:T(8,128)(2,1)S(1)} %bitcast.73) | data formatting | bytes 1048576 | tf_op jit(solution)/shard_map/stack;reshape | solution.py:78
  222.6 0.5 broadcast.90
  223.1 11.7 %reduce.3 = bf16[2048,128]{1,0:T(8,128)(2,1)S(1)} reduce(bf16[2048,1,128]{2,1,0:T(2,128)(2,1)S(1)} %bitcast.68, bf16[]{:T(256)} %broadcast.90), dimensions={1}, to_apply=%bitcast.58.reduce_sub_computation | reduce | bytes 1048578
  234.9 21.1 %all_to_all.26 = bf16[16,2,8192]{2,1,0:T(2,128)(2,1)S(1)} all-to-all(bf16[16,2,8192]{2,1,0:T(2,128)(2,1)S(1)} %reshape.115), channel_id=1, replica_groups=mesh['grp'=16,'sp'=16] {'sp'}, dimensions={0} | all-to-all | bytes 1048576 | tf_op jit(solution)/shard_map/all_to_all | solution.py:87
  256.0 0.5 reshape.116
  256.6 123.7 %all-gather.5.cloned.1.call-done = bf16[16,128,3072]{2,1,0:T(8,128)(2,1)} async-done(((bf16[1,128,3072]{2,1,0:T(8,128)(2,1)}), bf16[16,128,3072]{2,1,0:T(8,128)(2,1)}) %all-gather.5.cloned.1.call-update) | async-done | bytes 12582928 | tf_op jit(solution)/shard_map/all_gather | solution.py:77
  380.3 12.5 %convert_bitcast_fusion = bf16[1,128,16,3072]{3,1,2,0:T(8,128)(2,1)} fusion(bf16[128,16,128]{2,0,1:T(8,128)(2,1)S(1)} %bitcast.69, bf16[16,128,3072]{2,1,0:T(8,128)(2,1)} %all-gather.5.cloned.1.call-done), kind=kOutput, calls=%fused_computation.16 | convolution fusion | flops 1616904192 | bytes 25690112 | tf_op jit(solution)/shard_map/itnc,ncd->itnd/dot_general | solution.py:90
  392.8 7.5 %convert_reduce_fusion = f32[128,3072]{1,0:T(8,128)S(1)} fusion(bf16[1,128,16,3072]{3,1,2,0:T(8,128)(2,1)} %convert_bitcast_fusion), kind=kLoop, calls=%fused_computation.13 | loop fusion | flops 12189696 | bytes 14155776 | tf_op jit(solution)/shard_map/reduce_sum | solution.py:94
  400.3 1.0 fusion.24
  (21 shorter events, 0.6 us)
Async XLA Ops:
  6.5 3.9 copy-start
  6.5 187.3 %all-gather.3.cloned.1.call-start = ((), (), s32[]{:S(2)}) async-start(), calls=%async_computation.3 | async-start | bytes 13369344 | tf_op jit(solution)/shard_map/all_gather | solution.py:68
  7.3 5.0 %copy-start.2 = (bf16[1,8,3072]{2,1,0:T(8,128)(2,1)S(1)}, bf16[1,8,3072]{2,1,0:T(8,128)(2,1)}, u32[]{:S(2)}) copy-start(bf16[1,8,3072]{2,1,0:T(8,128)(2,1)} %param.11) | copy-start | bytes 147460
  10.4 21.7 %copy-start.1 = (bf16[1,192,384]{2,1,0:T(8,128)(2,1)S(1)}, bf16[1,192,384]{2,1,0:T(8,128)(2,1)}, u32[]{:S(2)}) copy-start(bf16[1,192,384]{2,1,0:T(8,128)(2,1)} %param.10) | copy-start | bytes 442372
  12.3 368.0 %all-gather.5.cloned.1.call-start = ((), (), s32[]{:S(2)}) async-start(), calls=%async_computation.4 | async-start | bytes 13369344 | tf_op jit(solution)/shard_map/all_gather | solution.py:77
  33.9 35.1 %all-to-all-start = ((bf16[16,1,192,384]{3,2,1,0:T(8,128)(2,1)}), bf16[16,1,192,384]{3,2,1,0:T(8,128)(2,1)S(1)}, u32[]{:S(2)}, u32[]{:S(2)}) async-start(bf16[16,1,192,384]{3,2,1,0:T(8,128)(2,1)} %broadcast_in_dim.10), calls=%async_computation | async-start | bytes 4718592 | tf_op jit(solution)/shard_map/all_to_all | solution.py:11
Sparse Core Ops, SparseCore 0:
  12.4 181.3 all-gather.2
  196.5 183.8 all-gather.4
where the time goes:
time: 408 us
  waiting for transfers between devices  279 us (68%)
  blocking collectives  40.7 us (10%)
  matrix products  32.4 us (8%)
  other arithmetic  25.4 us (6%)
  between operations  14.3 us (4%)
  local copies, waits for them, and re-layouts  11.5 us (3%)
  starting transfers between devices  4.48 us (1%)
    all_gather x1, waiting for transfers between devices, on_device(): whole = lax.all_gather(normed, 'sp', axis=1, tiled=True)  125 us
    all_gather x1, waiting for transfers between devices, on_device(): every_head = lax.all_gather(out_rows, 'sp', axis=0, tiled=True)  124 us
    all_to_all x1, waiting for transfers between devices, sent_to_all(): return lax.all_to_all(copies, axis, split_axis=0, concat_axis=0, tiled=True)  30.7 us
    all_to_all x1, blocking collectives, on_device(): lax.all_to_all(attended, 'sp', split_axis=1, concat_axis=2, tiled=True)  21.1 us
    all_to_all x1, blocking collectives, sent_to_all(): return lax.all_to_all(copies, axis, split_axis=0, concat_axis=0, tiled=True)  19.6 us
    dot_general x1, matrix products, on_device(): jnp.einsum('itnc,ncd->itnd', mixed, every_head, preferred_element_type=jn...  12.5 us
    unnamed x1, other arithmetic  11.7 us
    dot_general x1, matrix products, on_device(): jnp.einsum('itc,cf->itf', whole, gathered_copies(w_qkv, 'grp', 1)[0], pre...  9.63 us
  transfers between devices with their start and end apart: 3, of which 3 were waited for; matrix products, arithmetic and copies ran while one was open for 11% of the time, Pallas kernels for 0%

commit v1 on v0

v1 whole, which is shorter than its diff:
```python
import functools
import math

import jax
import jax.numpy as jnp
from jax import lax
from jax.experimental import pallas as pl
from jax.experimental.pallas import tpu as pltpu
from jax.sharding import PartitionSpec as P

MESH = pl.DeviceIdType.MESH
BF = jnp.bfloat16
F32 = jnp.float32

TR, TL, WX, WY, WD, OP, OZ, O1A, O1B, O2A, O2B, OD, KX, AZ, COUNT = (
    0, 7, 14, 18, 22, 26, 27, 35, 39, 43, 47, 51, 53, 61, 69,
)


def kernel(embed, lat_hbm, wm_hbm, wqkv_hbm, wout_hbm, out_hbm,
           xin, wm, mod, tok, wq, wo, pw_own, pw_par, qs, kv, at, mx, res,
           ss, rs, ls):
    s = lax.axis_index("sp")
    g = lax.axis_index("grp")
    z, xh = lax.div(s, 2), lax.rem(s, 2)
    xl, y, core = lax.div(g, 8), lax.rem(lax.div(g, 2), 4), lax.rem(g, 2)
    x = xh * 2 + xl

    def dev(zz, xx, yy, cc):
        grp = (lax.rem(xx, 2) * 4 + yy) * 2 + cc
        return (grp, zz * 2 + lax.div(xx, 2))

    zpeer = {o: dev(lax.rem(z + o, 8), x, y, core) for o in range(1, 8)}
    xpeer = {o: dev(z, lax.rem(x + o, 4), y, core) for o in range(1, 4)}
    ypeer = {o: dev(z, x, lax.rem(y + o, 4), core) for o in range(1, 4)}
    partner = dev(z, x, y, 1 - core)
    right, left = zpeer[1], zpeer[7]

    def rc(src, dst, i, to):
        return pltpu.make_async_remote_copy(
            src_ref=src, dst_ref=dst, send_sem=ss.at[i], recv_sem=rs.at[i],
            device_id=to, device_id_type=MESH,
        )

    sent = []

    def send(*args):
        copy = rc(*args)
        copy.start()
        sent.append(copy)
        return copy

    cols = pl.ds(pl.multiple_of(xh * 384, 128), 384)
    own_w = wq.at[xl, y, core, :, cols]

    c_w = pltpu.make_async_copy(wqkv_hbm, own_w, ls.at[0])
    c_o = pltpu.make_async_copy(wout_hbm, pw_own, ls.at[1])
    c_x = pltpu.make_async_copy(lat_hbm, xin, ls.at[2])
    c_m = pltpu.make_async_copy(wm_hbm.at[:, pl.ds(0, 6144)], wm.at[:, pl.ds(0, 6144)], ls.at[3])
    c_g = pltpu.make_async_copy(wm_hbm.at[:, pl.ds(6144, 3072)], wm.at[:, pl.ds(6144, 3072)], ls.at[4])
    for c in (c_w, c_o, c_m, c_x, c_g):
        c.start()

    barrier = pltpu.get_barrier_semaphore()
    for p in (*zpeer.values(), *xpeer.values(), *ypeer.values(), partner):
        pl.semaphore_signal(barrier, inc=1, device_id=p, device_id_type=MESH)
    c_w.wait()
    c_o.wait()
    pl.semaphore_wait(barrier, 14)

    wx = [send(own_w, own_w, WX + o, xpeer[o]) for o in (1, 3, 2)]
    op = send(pw_own, pw_par, OP, partner)

    def modulate(lo, hi):
        for j in range(lo, hi):
            mod[j] = jnp.dot(embed[...], wm[:, j * 768:(j + 1) * 768], preferred_element_type=F32)

    c_m.wait()
    modulate(0, 8)
    c_x.wait()

    op.wait_recv()
    first = core == 0
    for j in range(2):
        def half(ref):
            a = ref[:, j * 768:(j + 1) * 768].astype(F32)
            b = ref[:, 1536 + j * 768:1536 + (j + 1) * 768].astype(F32)
            return jnp.where(first, a, b)
        a, b = half(pw_own), half(pw_par)
        rows = jnp.concatenate([jnp.where(first, a, b), jnp.where(first, b, a)], axis=0)
        wo[core * 2 + j, z, xh, xl, y] = rows.astype(BF)
    own_o = wo.at[pl.ds(core * 2, 2), z, xh, xl, y]
    oz = [send(own_o, own_o, OZ + o, zpeer[o]) for o in (4, 3, 5, 2, 6, 1, 7)]

    def norm_rows(i, carry):
        r = pl.ds(pl.multiple_of(i * 16, 16), 16)
        v = xin[r, :].astype(F32)
        center = jnp.sum(v, axis=-1, keepdims=True) * (1.0 / 3072)
        v = v - center
        spread = jnp.sum(v * v, axis=-1, keepdims=True) * (1.0 / 3072)
        v = v * lax.rsqrt(spread + 1e-06)
        for j in range(4):
            c = slice(j * 768, (j + 1) * 768)
            tok[0, r, c] = (v[:, c] * (1.0 + mod[4 + j]) + mod[j]).astype(BF)
        return carry

    part = (pl.ds(0, 64), pl.ds(64, 64))

    def tright(k):
        d, c = k // 2, k % 2
        return send(tok.at[d, part[c]], tok.at[d + 1, part[c]], TR + k, right)

    def tleft(k):
        d, c = k // 2, 1 - k % 2
        return send(tok.at[(8 - d) % 8, part[c]], tok.at[7 - d, part[c]], TL + k, left)

    tr, tl = {}, {}
    lax.fori_loop(0, 4, norm_rows, 0)
    tr[0] = tright(0)
    lax.fori_loop(4, 8, norm_rows, 0)
    tl[0] = tleft(0)
    tr[1] = tright(1)
    tl[1] = tleft(1)

    c_g.wait()
    modulate(8, 12)

    for c in wx:
        c.wait_recv()
    for c in oz:
        c.wait_recv()

    def sub(j):
        return wo.at[core * 2 + j, :, xh, xl, y]

    o1a = [send(sub(0), sub(0), O1A + o, xpeer[o]) for o in (1, 3, 2)]
    o1b = [send(sub(1), sub(1), O1B + o, ypeer[o]) for o in (1, 3, 2)]
    yrow = wq.at[:, y, core]
    wy = {o: send(yrow, yrow, WY + o, ypeer[o]) for o in (1, 3, 2)}
    wd = [send(yrow, yrow, WD, partner)]

    def project(slot):
        acc = jnp.zeros((128, 768), F32)
        for a in range(2):
            w = wq[a].reshape(1536, 768)
            acc += jnp.dot(tok[slot, :, a * 1536:(a + 1) * 1536], w, preferred_element_type=F32)
        acc = acc.astype(BF)
        qs[slot, :, 0:128] = acc[:, 0:128]
        qs[slot, :, 128:256] = acc[:, 384:512]
        kv[slot, :, 0:256] = acc[:, 128:384]
        kv[slot, :, 256:512] = acc[:, 512:768]
        rc(kv.at[slot], kv.at[8 + slot], KX + slot, xpeer[2]).start()

    def project_some(count, slot_of):
        def body(i, carry):
            project(slot_of(i))
            return carry
        lax.fori_loop(0, count, body, 0)

    def od(j):
        ref = wo.at[core * 2 + j]
        return send(ref, ref, OD + j, partner)

    for k in range(7):
        tr[k].wait_recv()
        if k < 5:
            tr[k + 2] = tright(k + 2)
        tl[k].wait_recv()
        if k < 5:
            tl[k + 2] = tleft(k + 2)
        if k == 1:
            for c in o1a:
                c.wait_recv()
            ref = wo.at[core * 2, :, :, :, y]
            o2a = [send(ref, ref, O2A + o, ypeer[o]) for o in (1, 3, 2)]
            for c in o1b:
                c.wait_recv()
            ref = wo.at[core * 2 + 1, :, xh, xl]
            ref1 = wo.at[core * 2 + 1, :, xh, xl]
            o2b = [send(ref, ref1, O2B + o, xpeer[o]) for o in (1, 3, 2)]
        if k == 3:
            for i, o in enumerate((1, 3, 2)):
                wy[o].wait_recv()
                ref = wq.at[:, lax.rem(y + 4 - o, 4), core]
                wd.append(send(ref, ref, WD + o, partner))
            for c in wd:
                c.wait_recv()
            project_some(5, lambda i: lax.rem(i + 6, 8))
        if k == 5:
            project_some(2, lambda i: 3 + 2 * i)
        if k == 6:
            project_some(1, lambda i: i + 4)

    for slot in range(8):
        rc(kv.at[slot], kv.at[8 + slot], KX + slot, xpeer[2]).wait_recv()

    unit = 1.0 / math.sqrt(128)

    def attend(i, carry):
        a, b = 4 + i, 3 - i
        for h in range(2):
            hc = slice(h * 128, (h + 1) * 128)
            q = jnp.concatenate([qs[a, :, hc], qs[b, :, hc]], axis=0)
            keys = kv[:, :, h * 256:h * 256 + 128].reshape(2048, 128)
            vals = kv[:, :, h * 256 + 128:h * 256 + 256].reshape(2048, 128)
            sc = lax.dot_general(q, keys, (((1,), (1,)), ((), ())), preferred_element_type=F32)
            top = jnp.max(sc, axis=1, keepdims=True)
            e = jnp.exp((sc - top) * unit)
            total = jnp.sum(e, axis=1, keepdims=True)
            o = jnp.dot(e.astype(BF), vals, preferred_element_type=F32) / total
            o = o.astype(BF)
            at[a, :, hc] = o[:128]
            at[b, :, hc] = o[128:]
        rc(at.at[a], mx.at[z], AZ + a, dev(lax.rem(z + 8 - a, 8), x, y, core)).start()

        @pl.when(i < 3)
        def _():
            rc(at.at[b], mx.at[z], AZ + b, dev(lax.rem(z + 8 - b, 8), x, y, core)).start()

        return carry

    lax.fori_loop(0, 4, attend, 0)
    mx[z] = at[0]

    for c in o2a:
        c.wait_recv()
    od0 = od(0)
    for c in o2b:
        c.wait_recv()
    od1 = od(1)
    az = [rc(at.at[d], mx.at[z], AZ + d, dev(lax.rem(z + 8 - d, 8), x, y, core)) for d in range(1, 8)]
    for c in az:
        c.wait_recv()

    def out_copy(q):
        return pltpu.make_async_copy(
            res.at[q], out_hbm.at[:, pl.ds(pl.multiple_of(q * 768, 128), 768)], ls.at[q])

    def out_part(i, carry):
        q = lax.rem(core * 2 + i, 4)
        m = jnp.concatenate([mx[k] for k in range(8)], axis=1)
        acc = jnp.dot(m, wo[q].reshape(2048, 768), preferred_element_type=F32)
        res[q] = (acc * mod[8 + q][0:1]).astype(BF)
        out_copy(q).start()
        return carry

    lax.fori_loop(0, 2, out_part, 0)
    od0.wait_recv()
    od1.wait_recv()
    lax.fori_loop(2, 4, out_part, 0)

    for q in range(4):
        out_copy(q).wait()
    for c in sent:
        c.wait_send()
    for slot in range(8):
        rc(kv.at[slot], kv.at[8 + slot], KX + slot, xpeer[2]).wait_send()
    for c in az:
        c.wait_send()


def on_device(latents, timestep, w_mod, w_qkv, w_out):
    half_freq = w_mod.shape[0] // 2
    freqs = jnp.exp(-math.log(10000.0) * jnp.arange(half_freq, dtype=F32) / half_freq)
    angles = timestep.astype(F32)[:, None] * freqs[None, :]
    embed = jnp.concatenate([jnp.cos(angles), jnp.sin(angles)], axis=1).astype(BF)
    embed = jnp.broadcast_to(embed, (16, 2 * half_freq))
    anyspace = pl.BlockSpec(memory_space=pl.ANY)
    out = pl.pallas_call(
        kernel,
        out_shape=jax.ShapeDtypeStruct((128, 3072), BF),
        in_specs=[pl.BlockSpec(memory_space=pltpu.VMEM)] + [anyspace] * 4,
        out_specs=anyspace,
        scratch_shapes=[
            pltpu.VMEM((128, 3072), BF),
            pltpu.VMEM((256, 9216), BF),
            pltpu.VMEM((12, 16, 768), F32),
            pltpu.VMEM((8, 128, 3072), BF),
            pltpu.VMEM((2, 4, 2, 192, 768), BF),
            pltpu.VMEM((4, 8, 2, 2, 4, 16, 768), BF),
            pltpu.VMEM((8, 3072), BF),
            pltpu.VMEM((8, 3072), BF),
            pltpu.VMEM((8, 128, 256), BF),
            pltpu.VMEM((16, 128, 512), BF),
            pltpu.VMEM((8, 128, 256), BF),
            pltpu.VMEM((8, 128, 256), BF),
            pltpu.VMEM((4, 128, 768), BF),
            pltpu.SemaphoreType.DMA((COUNT,)),
            pltpu.SemaphoreType.DMA((COUNT,)),
            pltpu.SemaphoreType.DMA((5,)),
        ],
        compiler_params=pltpu.CompilerParams(
            collective_id=0, has_side_effects=True, vmem_limit_bytes=60 * 1024 * 1024,
        ),
        name="sublayer",
    )(embed, latents[0], w_mod, w_qkv[0], w_out[0])
    return out[None]


def solution(mesh):
    placed = (P("grp", "sp", None), P("grp"), P(), P("sp", "grp", None), P("sp", "grp", None))
    return jax.shard_map(
        on_device, mesh=mesh, in_specs=placed, out_specs=P("grp", "sp", None), check_vma=False
    )
```

time: 408 us -> 123 us (0.30)
  waiting for transfers between devices: 279 us -> 0 us
  Pallas kernels: 0 us -> 120 us
  blocking collectives: 40.7 us -> 0 us
  matrix products: 32.4 us -> 0 us
  other arithmetic: 25.4 us -> 0.06 us
  between operations: 14.3 us -> 0.67 us
  local copies, waits for them, and re-layouts: 11.5 us -> 2.67 us
  starting transfers between devices: 4.48 us -> 0 us
    all_gather x2 -> x0, waiting for transfers between devices: 249 us -> none  [the longest x1 125 us: on_device(): whole = lax.all_gather(normed, 'sp', axis=1, tiled=True)]
    pallas_call x0 -> x1, Pallas kernels: none -> 120 us  [on_device(): pl.pallas_call(kernel, out_shape=jax.ShapeDtypeStruct((128, 3072), BF), i...]
    all_to_all x2 -> x0, blocking collectives: 40.7 us -> none  [the longest x1 21.1 us: on_device(): lax.all_to_all(attended, 'sp', split_axis=1, concat_axis=2, tiled=True)]
    dot_general x11 -> x0, matrix products: 32.4 us -> none  [the longest x1 12.5 us: on_device(): jnp.einsum('itnc,ncd->itnd', mixed, every_head, preferred_element_type=jn...]
    all_to_all x1 -> x0, waiting for transfers between devices: 30.7 us -> none  [sent_to_all(): return lax.all_to_all(copies, axis, split_axis=0, concat_axis=0, tiled=True)]
    unnamed x1 -> x0, other arithmetic: 11.7 us -> none
    reduce_sum x7 -> x0, other arithmetic: 11.3 us -> none  [the longest x1 7.48 us: on_device(): total = jnp.sum(contrib.astype(jnp.float32), axis=2)]
    another operation x1 -> x0, local copies, waits for them, and re-layouts: 8.14 us -> none  [on_device(): jnp.stack([attend(qkv[0, :, :head_size], qkv[0, :, head_size:2 * head_siz...]
  transfers between devices with their start and end apart: 3 -> 0, of which waited for: 3 -> 0; matrix products, arithmetic and copies ran while one was open for 11% -> 0% of each run, Pallas kernels for 0% -> 0%
where the time goes in v1:
time: 123 us
  Pallas kernels  120 us (98%)
  local copies, waits for them, and re-layouts  2.67 us (2%)
    pallas_call x1, Pallas kernels, on_device(): pl.pallas_call(kernel, out_shape=jax.ShapeDtypeStruct((128, 3072), BF), i...  120 us

profile of v1, /device:TPU:1, one launch (start us, length us, event | category | flops | bytes accessed | tf_op | source)
XLA Modules:
  0.0 123.1 jit_solution(4193107085850920485)
XLA Ops:
  0.7 0.1 sine_convert_fusion
  0.7 0.6 broadcast_in_dim.4.embed
  1.3 119.7 %sublayer.1 = bf16[128,3072]{1,0:T(8,128)(2,1)} custom-call(bf16[16,256]{1,0:T(8,128)(2,1)} %broadcast_in_dim.4.embed, bf16[128,3072]{1,0:T(8,128)(2,1)} %bitcast.6, bf16[256,9216]{1,0:T(8,128)(2,1)} %wm_hbm.1, bf16[192,384]{1,0:T(8,128)(2,1)} %bitcast.7, bf16[8,3072]{1,0:T(8,128)(2,1)} %bitcast.8), custom_call_target="tpu_custom_call" | custom-call | tf_op jit(solution)/shard_map/sublayer/pallas_call | solution.py:269
  121.0 2.1 %copy.8 = bf16[1,128,3072]{2,1,0:T(8,128)(2,1)} copy(bf16[1,128,3072]{2,1,0:T(8,128)(2,1)} %bitcast.5) | data formatting | bytes 1572864
  (1 shorter events, 0.0 us)

commit v2 on v1

v2 whole, which is shorter than its diff:
```python
import functools
import math

import jax
import jax.numpy as jnp
from jax import lax
from jax.experimental import pallas as pl
from jax.experimental.pallas import tpu as pltpu
from jax.sharding import PartitionSpec as P

MESH = pl.DeviceIdType.MESH
BF = jnp.bfloat16
F32 = jnp.float32

TR, TL, WXA, WYA, WYB, WXB, WD, OP, OZR, OZL = 0, 7, 14, 18, 24, 28, 34, 50, 51, 56
AX, AY, BX, BY, CX, CY, OD, KX, AZ, COUNT = 61, 65, 71, 75, 81, 85, 91, 115, 123, 131

PLACE = (0, 1, 3, 5, 7, 6, 4, 2)


class Direct:
    def __init__(self, send, ref, base, peers):
        self.copies = [send(ref, ref, base + o, peers[o]) for o in (2, 1, 3)]

    def finish(self):
        for c in self.copies:
            c.wait_recv()


class Ring:
    def __init__(self, send, region, me, base, plus, minus, landed=None):
        self.send, self.region, self.base = send, region, base
        self.me, self.plus, self.minus = me, plus, minus
        self.landed = landed
        self.copies = {}
        for k, half, to in ((0, 0, plus), (2, 1, minus), (1, 1, plus), (3, 0, minus)):
            self.go(k, 0, half, to)
        if landed:
            landed(me, 0, 0)
            landed(me, 1, 1)

    def go(self, k, shift, half, to):
        ref = self.region(lax.rem(self.me + shift, 4), half)
        self.copies[k] = self.send(ref, ref, self.base + k, to)

    def arrive(self, k, shift, half, n):
        self.copies[k].wait_recv()
        if self.landed:
            self.landed(lax.rem(self.me + shift, 4), half, n)

    def forward(self):
        self.copies[0].wait_recv()
        self.go(4, 3, 0, self.plus)
        self.copies[2].wait_recv()
        self.go(5, 1, 1, self.minus)
        if self.landed:
            self.landed(lax.rem(self.me + 3, 4), 0, 2)
            self.landed(lax.rem(self.me + 1, 4), 1, 3)

    def near(self):
        self.arrive(1, 3, 1, 4)
        self.arrive(3, 1, 0, 5)

    def far(self):
        self.arrive(4, 2, 0, 6)
        self.arrive(5, 2, 1, 7)

    def finish(self):
        self.near()
        self.far()


def kernel(embed, lat_hbm, wm_hbm, wqkv_hbm, wout_hbm, out_hbm,
           wm, mod, tok, nrm, wq, wo, pw_own, pw_par, qs, kv, at, mx, acc, res,
           ss, rs, ls):
    s = lax.axis_index("sp")
    g = lax.axis_index("grp")
    z, xh = lax.div(s, 2), lax.rem(s, 2)
    xl, y, core = lax.div(g, 8), lax.rem(lax.div(g, 2), 4), lax.rem(g, 2)
    x = xh * 2 + xl

    def dev(zz, xx, yy, cc):
        grp = (lax.rem(xx, 2) * 4 + yy) * 2 + cc
        return (grp, zz * 2 + lax.div(xx, 2))

    zpeer = {o: dev(lax.rem(z + o, 8), x, y, core) for o in range(1, 8)}
    xpeer = {o: dev(z, lax.rem(x + o, 4), y, core) for o in range(1, 4)}
    ypeer = {o: dev(z, x, lax.rem(y + o, 4), core) for o in range(1, 4)}
    partner = dev(z, x, y, 1 - core)
    right, left = zpeer[1], zpeer[7]

    def rc(src, dst, i, to):
        return pltpu.make_async_remote_copy(
            src_ref=src, dst_ref=dst, send_sem=ss.at[i], recv_sem=rs.at[i],
            device_id=to, device_id_type=MESH,
        )

    sent = []

    def send(*args):
        copy = rc(*args)
        copy.start()
        sent.append(copy)
        return copy

    cols = pl.ds(pl.multiple_of(xh * 384, 128), 384)
    own_w = wq.at[xl, y, core, :, cols]

    c_w = pltpu.make_async_copy(wqkv_hbm, own_w, ls.at[0])
    c_o = pltpu.make_async_copy(wout_hbm, pw_own, ls.at[1])
    c_x = pltpu.make_async_copy(lat_hbm, tok.at[0], ls.at[2])
    c_m = pltpu.make_async_copy(wm_hbm, wm, ls.at[3])
    for c in (c_x, c_w, c_o, c_m):
        c.start()

    barrier = pltpu.get_barrier_semaphore()
    for p in (*zpeer.values(), *xpeer.values(), *ypeer.values(), partner):
        pl.semaphore_signal(barrier, inc=1, device_id=p, device_id_type=MESH)
    c_x.wait()
    c_w.wait()
    c_o.wait()
    pl.semaphore_wait(barrier, 14)

    part = (pl.ds(0, 64), pl.ds(64, 64))

    def tright(k):
        d, c = k // 2, k % 2
        return send(tok.at[d, part[c]], tok.at[d + 1, part[c]], TR + k, right)

    def tleft(k):
        d, c = k // 2, 1 - k % 2
        return send(tok.at[(8 - d) % 8, part[c]], tok.at[7 - d, part[c]], TL + k, left)

    tr, tl = {0: tright(0)}, {0: tleft(0)}

    op = send(pw_own, pw_par, OP, partner)
    top, low = pl.ds(0, 96), pl.ds(96, 96)
    wxa = Direct(send, wq.at[xl, y, core, top, cols], WXA, xpeer)
    wyb = Direct(send, wq.at[xl, y, core, low, cols], WYB, ypeer)

    op.wait_recv()
    first = core == 0
    for j in range(2):
        def half(ref):
            a = ref[:, j * 768:(j + 1) * 768].astype(F32)
            b = ref[:, 1536 + j * 768:1536 + (j + 1) * 768].astype(F32)
            return jnp.where(first, a, b)
        a, b = half(pw_own), half(pw_par)
        rows = jnp.concatenate([jnp.where(first, a, b), jnp.where(first, b, a)], axis=0)
        wo[core * 2 + j, 0, xh, xl, y] = rows.astype(BF)

    def slab(slot, far):
        quarter = pl.ds(core * 2, 2) if far is None else core * 2 + far
        return wo.at[quarter, PLACE[slot], xh, xl, y]

    def hop(h):
        r, l = (0, 1) if h == 4 else (None, None)
        return (send(slab(h - 1, r), slab(h, r), OZR + h, right),
                send(slab((9 - h) % 8, l), slab(8 - h, l), OZL + h, left))

    oz = {1: hop(1)}
    tr[1] = tright(1)
    tl[1] = tleft(1)

    c_m.wait()
    for j in range(12):
        mod[j] = jnp.dot(embed[...], wm[:, j * 768:(j + 1) * 768], preferred_element_type=F32)

    def normalize(slot):
        def rows(i, carry):
            r = pl.ds(pl.multiple_of(i * 16, 16), 16)
            v = tok[slot, r, :].astype(F32)
            center = jnp.sum(v, axis=-1, keepdims=True) * (1.0 / 3072)
            v = v - center
            spread = jnp.sum(v * v, axis=-1, keepdims=True) * (1.0 / 3072)
            v = v * lax.rsqrt(spread + 1e-06)
            for j in range(4):
                c = slice(j * 768, (j + 1) * 768)
                nrm[slot, r, c] = (v[:, c] * (1.0 + mod[4 + j]) + mod[j]).astype(BF)
            return carry
        lax.fori_loop(0, 8, rows, 0)

    wd = []

    def wya_region(i, h):
        return wq.at[h, i, core, top]

    def wxb_region(i, h):
        c = pl.ds(pl.multiple_of(lax.div(i, 2) * 384, 128), 384)
        return wq.at[lax.rem(i, 2), pl.ds(h * 2, 2), core, low, c]

    def w_landed(region, base):
        def landed(i, h, n):
            ref = region(i, h)
            wd.append(send(ref, ref, base + n, partner))
        return landed

    wxa.finish()
    wya = Ring(send, wya_region, y, WYA, ypeer[1], ypeer[3], w_landed(wya_region, WD))
    wyb.finish()
    wxb = Ring(send, wxb_region, x, WXB, xpeer[1], xpeer[3], w_landed(wxb_region, WD + 8))
    normalize(0)

    groups = {"a": pl.ds(0, 3), "b": pl.ds(3, 2), "c": pl.ds(5, 3)}
    od = []

    def one(name, base):
        return Direct(send, wo.at[pl.ds(core * 2, 2), groups[name], xh, xl, y], base, xpeer)

    def two(name, base, first_od):
        def region(i, h):
            return wo.at[core * 2 + h, groups[name], :, :, i]

        def landed(i, h, n):
            ref = region(i, h)
            od.append(send(ref, ref, OD + first_od + n, partner))

        return Ring(send, region, y, base, ypeer[1], ypeer[3], landed)

    def project(slot):
        acc = jnp.zeros((128, 768), F32)
        for a in range(2):
            w = wq[a].reshape(1536, 768)
            acc += jnp.dot(nrm[slot, :, a * 1536:(a + 1) * 1536], w, preferred_element_type=F32)
        acc = acc.astype(BF)
        qs[slot, :, 0:128] = acc[:, 0:128]
        qs[slot, :, 128:256] = acc[:, 384:512]
        kv[slot, :, 0:256] = acc[:, 128:384]
        kv[slot, :, 256:512] = acc[:, 512:768]
        rc(kv.at[slot], kv.at[8 + slot], KX + slot, xpeer[2]).start()

    def project_some(count, slot_of):
        def body(i, carry):
            project(slot_of(i))
            return carry
        lax.fori_loop(0, count, body, 0)

    for k in range(7):
        tr[k].wait_recv()
        tl[k].wait_recv()
        if k < 4:
            for c in oz[k + 1]:
                c.wait_recv()
            if k < 3:
                oz[k + 2] = hop(k + 2)
        if k < 5:
            tr[k + 2] = tright(k + 2)
            tl[k + 2] = tleft(k + 2)
        if k == 0:
            ax = one("a", AX)
            wya.forward()
            wxb.forward()
        if k == 1:
            bx = one("b", BX)
            ax.finish()
            ay = two("a", AY, 0)
            normalize(1)
            normalize(7)
            wya.finish()
            wxb.finish()
        if k == 2:
            bx.finish()
            by = two("b", BY, 8)
            for c in wd:
                c.wait_recv()
            project_some(3, lambda i: lax.rem(i + 7, 8))
        if k == 3:
            cx = one("c", CX)
            ay.forward()
            normalize(2)
            normalize(6)
            project_some(2, lambda i: 2 + 4 * i)
        if k == 4:
            by.forward()
            cx.finish()
            cy = two("c", CY, 16)
        if k == 5:
            ay.finish()
            normalize(3)
            normalize(5)
            project_some(2, lambda i: 3 + 2 * i)
        if k == 6:
            normalize(4)
            project_some(1, lambda i: i + 4)
            cy.forward()
            by.finish()

    for slot in range(8):
        rc(kv.at[slot], kv.at[8 + slot], KX + slot, xpeer[2]).wait_recv()

    unit = 1.0 / math.sqrt(128)

    def attend(i, carry):
        a, b = 4 + i, 3 - i
        for h in range(2):
            hc = slice(h * 128, (h + 1) * 128)
            q = jnp.concatenate([qs[a, :, hc], qs[b, :, hc]], axis=0)
            keys = kv[:, :, h * 256:h * 256 + 128].reshape(2048, 128)
            vals = kv[:, :, h * 256 + 128:h * 256 + 256].reshape(2048, 128)
            sc = lax.dot_general(q, keys, (((1,), (1,)), ((), ())), preferred_element_type=F32)
            top = jnp.max(sc, axis=1, keepdims=True)
            e = jnp.exp((sc - top) * unit)
            total = jnp.sum(e, axis=1, keepdims=True)
            o = jnp.dot(e.astype(BF), vals, preferred_element_type=F32) / total
            o = o.astype(BF)
            at[a, :, hc] = o[:128]
            at[b, :, hc] = o[128:]
        rc(at.at[a], mx.at[8 - a], AZ + a, dev(lax.rem(z + 8 - a, 8), x, y, core)).start()

        @pl.when(i < 3)
        def _():
            rc(at.at[b], mx.at[8 - b], AZ + b, dev(lax.rem(z + 8 - b, 8), x, y, core)).start()

        return carry

    lax.fori_loop(0, 4, attend, 0)
    mx[0] = at[0]

    az = {d: rc(at.at[d], mx.at[8 - d], AZ + d, dev(lax.rem(z + 8 - d, 8), x, y, core)) for d in range(1, 8)}

    def out_copy(q):
        return pltpu.make_async_copy(
            res.at[q], out_hbm.at[:, pl.ds(q * 768, 768)], ls.at[q])

    cy.finish()
    for c in od:
        c.wait_recv()
    for n, pair in enumerate(((4, 3), (5, 2), (6, 1), (7, 0))):
        for d in pair:
            if d > 0:
                az[d].wait_recv()
        ta, tb = ((8 - d) % 8 for d in pair)
        pa, pb = PLACE[ta], PLACE[tb]

        def out_part(q, carry):
            m = jnp.concatenate([mx[ta], mx[tb]], axis=1)
            w = jnp.concatenate([wo[q, pa].reshape(256, 768), wo[q, pb].reshape(256, 768)], axis=0)
            part_sum = jnp.dot(m, w, preferred_element_type=F32)
            if n > 0:
                part_sum += acc[q]
            if n < 3:
                acc[q] = part_sum
            else:
                res[q] = (part_sum * mod[8 + q][0:1]).astype(BF)
            return carry

        if n < 3:
            lax.fori_loop(0, 4, out_part, 0)
        else:
            for q in range(4):
                out_part(q, 0)
                out_copy(q).start()

    for q in range(4):
        out_copy(q).wait()
    for c in sent:
        c.wait_send()
    for slot in range(8):
        rc(kv.at[slot], kv.at[8 + slot], KX + slot, xpeer[2]).wait_send()
    for c in az.values():
        c.wait_send()


def on_device(latents, timestep, w_mod, w_qkv, w_out):
    half_freq = w_mod.shape[0] // 2
    freqs = jnp.exp(-math.log(10000.0) * jnp.arange(half_freq, dtype=F32) / half_freq)
    angles = timestep.astype(F32)[:, None] * freqs[None, :]
    embed = jnp.concatenate([jnp.cos(angles), jnp.sin(angles)], axis=1).astype(BF)
    embed = jnp.broadcast_to(embed, (16, 2 * half_freq))
    anyspace = pl.BlockSpec(memory_space=pl.ANY)
    out = pl.pallas_call(
        kernel,
        out_shape=jax.ShapeDtypeStruct((128, 3072), BF),
        in_specs=[pl.BlockSpec(memory_space=pltpu.VMEM)] + [anyspace] * 4,
        out_specs=anyspace,
        scratch_shapes=[
            pltpu.VMEM((256, 9216), BF),
            pltpu.VMEM((12, 16, 768), F32),
            pltpu.VMEM((8, 128, 3072), BF),
            pltpu.VMEM((8, 128, 3072), BF),
            pltpu.VMEM((2, 4, 2, 192, 768), BF),
            pltpu.VMEM((4, 8, 2, 2, 4, 16, 768), BF),
            pltpu.VMEM((8, 3072), BF),
            pltpu.VMEM((8, 3072), BF),
            pltpu.VMEM((8, 128, 256), BF),
            pltpu.VMEM((16, 128, 512), BF),
            pltpu.VMEM((8, 128, 256), BF),
            pltpu.VMEM((8, 128, 256), BF),
            pltpu.VMEM((4, 128, 768), F32),
            pltpu.VMEM((4, 128, 768), BF),
            pltpu.SemaphoreType.DMA((COUNT,)),
            pltpu.SemaphoreType.DMA((COUNT,)),
            pltpu.SemaphoreType.DMA((5,)),
        ],
        compiler_params=pltpu.CompilerParams(
            collective_id=0, has_side_effects=True, vmem_limit_bytes=60 * 1024 * 1024,
        ),
        name="sublayer",
    )(embed, latents[0], w_mod, w_qkv[0], w_out[0])
    return out[None]


def solution(mesh):
    placed = (P("grp", "sp", None), P("grp"), P(), P("sp", "grp", None), P("sp", "grp", None))
    return jax.shard_map(
        on_device, mesh=mesh, in_specs=placed, out_specs=P("grp", "sp", None), check_vma=False
    )
```

time: 123 us -> 104 us (0.85)
  Pallas kernels: 120 us -> 101 us
    pallas_call x1, Pallas kernels: 120 us -> 101 us  [on_device(): pl.pallas_call(kernel, out_shape=jax.ShapeDtypeStruct((128, 3072), BF), i...]
where the time goes in v2:
time: 104 us
  Pallas kernels  101 us (97%)
  local copies, waits for them, and re-layouts  2.67 us (3%)
    pallas_call x1, Pallas kernels, on_device(): pl.pallas_call(kernel, out_shape=jax.ShapeDtypeStruct((128, 3072), BF), i...  101 us

profile of v2, /device:TPU:1, one launch (start us, length us, event | category | flops | bytes accessed | tf_op | source)
XLA Modules:
  0.0 103.9 jit_solution(9112694735710278981)
XLA Ops:
  0.7 0.1 sine_convert_fusion
  0.7 0.6 broadcast_in_dim.4.embed
  1.3 100.5 %sublayer.1 = bf16[128,3072]{1,0:T(8,128)(2,1)} custom-call(bf16[16,256]{1,0:T(8,128)(2,1)} %broadcast_in_dim.4.embed, bf16[128,3072]{1,0:T(8,128)(2,1)} %bitcast.6, bf16[256,9216]{1,0:T(8,128)(2,1)} %wm_hbm.1, bf16[192,384]{1,0:T(8,128)(2,1)} %bitcast.7, bf16[8,3072]{1,0:T(8,128)(2,1)} %bitcast.8), custom_call_target="tpu_custom_call" | custom-call | tf_op jit(solution)/shard_map/sublayer/pallas_call | solution.py:371
  101.8 2.1 %copy.8 = bf16[1,128,3072]{2,1,0:T(8,128)(2,1)} copy(bf16[1,128,3072]{2,1,0:T(8,128)(2,1)} %bitcast.5) | data formatting | bytes 1572864
  (1 shorter events, 0.0 us)

commit v3 on v2

--- a/solution.py
+++ b/solution.py
@@ -12,8 +12,8 @@
 BF = jnp.bfloat16
 F32 = jnp.float32
 
-TR, TL, WXA, WYA, WYB, WXB, WD, OP, OZR, OZL = 0, 7, 14, 18, 24, 28, 34, 50, 51, 56
-AX, AY, BX, BY, CX, CY, OD, KX, AZ, COUNT = 61, 65, 71, 75, 81, 85, 91, 115, 123, 131
+TR, TL, WXA, WYA, WYB, WXB, WD, OP, OZR, OZL = 0, 8, 16, 20, 26, 30, 36, 52, 53, 58
+AX, AY, BX, BY, CX, CY, OD, KX, AZ, COUNT = 63, 67, 73, 77, 83, 87, 93, 117, 127, 135
 
 PLACE = (0, 1, 3, 5, 7, 6, 4, 2)
 
@@ -123,15 +123,26 @@
 
     part = (pl.ds(0, 64), pl.ds(64, 64))
 
-    def tright(k):
-        d, c = k // 2, k % 2
-        return send(tok.at[d, part[c]], tok.at[d + 1, part[c]], TR + k, right)
-
-    def tleft(k):
-        d, c = k // 2, 1 - k % 2
-        return send(tok.at[(8 - d) % 8, part[c]], tok.at[7 - d, part[c]], TL + k, left)
-
-    tr, tl = {0: tright(0)}, {0: tleft(0)}
+    def right_copy(k):
+        d = k // 2
+        rows = part[k % 2] if d < 3 else pl.ds(32 * (7 - k), 32)
+        return rc(tok.at[d, rows], tok.at[d + 1, rows], TR + k, right)
+
+    def left_copy(k):
+        d = k // 2
+        rows = part[1 - k % 2] if d < 3 else pl.ds(64 + 32 * (k - 6), 32)
+        return rc(tok.at[(8 - d) % 8, rows], tok.at[7 - d, rows], TL + k, left)
+
+    tr = {k: right_copy(k) for k in range(8)}
+    tl = {k: left_copy(k) for k in range(8)}
+    sent.extend([*tr.values(), *tl.values()])
+
+    def pass_on(k):
+        tr[k].start()
+        tl[k].start()
+
+    pass_on(0)
+
 
     op = send(pw_own, pw_par, OP, partner)
     top, low = pl.ds(0, 96), pl.ds(96, 96)
@@ -159,14 +170,16 @@
                 send(slab((9 - h) % 8, l), slab(8 - h, l), OZL + h, left))
 
     oz = {1: hop(1)}
-    tr[1] = tright(1)
-    tl[1] = tleft(1)
+
+    pass_on(1)
+
 
     c_m.wait()
+    wave = jnp.broadcast_to(embed[...].astype(F32), (16, 256)).astype(BF)
     for j in range(12):
-        mod[j] = jnp.dot(embed[...], wm[:, j * 768:(j + 1) * 768], preferred_element_type=F32)
-
-    def normalize(slot):
+        mod[j] = jnp.dot(wave, wm[:, j * 768:(j + 1) * 768], preferred_element_type=F32)
+
+    def normalize(slot, lo=0, hi=8):
         def rows(i, carry):
             r = pl.ds(pl.multiple_of(i * 16, 16), 16)
             v = tok[slot, r, :].astype(F32)
@@ -178,7 +191,7 @@
                 c = slice(j * 768, (j + 1) * 768)
                 nrm[slot, r, c] = (v[:, c] * (1.0 + mod[4 + j]) + mod[j]).astype(BF)
             return carry
-        lax.fori_loop(0, 8, rows, 0)
+        lax.fori_loop(lo, hi, rows, 0)
 
     wd = []
 
@@ -229,6 +242,28 @@
         kv[slot, :, 256:512] = acc[:, 512:768]
         rc(kv.at[slot], kv.at[8 + slot], KX + slot, xpeer[2]).start()
 
+    kv_last = {
+        r: rc(kv.at[4, pl.ds(r, n)], kv.at[12, pl.ds(r, n)], KX + i, xpeer[2])
+        for i, r, n in ((4, 32, 64), (8, 0, 32), (9, 96, 32))
+    }
+
+    def project_last(starts):
+        acc = jnp.zeros((64, 768), F32)
+        size = 64 // len(starts)
+        for a in range(2):
+            w = wq[a].reshape(1536, 768)
+            cut = slice(a * 1536, (a + 1) * 1536)
+            rows = jnp.concatenate([nrm[4, r:r + size, cut] for r in starts], axis=0)
+            acc += jnp.dot(rows, w, preferred_element_type=F32)
+        acc = acc.astype(BF)
+        for n, r in enumerate(starts):
+            one = acc[n * size:(n + 1) * size]
+            qs[4, r:r + size, 0:128] = one[:, 0:128]
+            qs[4, r:r + size, 128:256] = one[:, 384:512]
+            kv[4, r:r + size, 0:256] = one[:, 128:384]
+            kv[4, r:r + size, 256:512] = one[:, 512:768]
+            kv_last[r].start()
+
     def project_some(count, slot_of):
         def body(i, carry):
             project(slot_of(i))
@@ -244,8 +279,9 @@
             if k < 3:
                 oz[k + 2] = hop(k + 2)
         if k < 5:
-            tr[k + 2] = tright(k + 2)
-            tl[k + 2] = tleft(k + 2)
+            pass_on(k + 2)
+        if k == 4:
+            pass_on(7)
         if k == 0:
             ax = one("a", AX)
             wya.forward()
@@ -279,19 +315,26 @@
             normalize(3)
             normalize(5)
             project_some(2, lambda i: 3 + 2 * i)
+            cy.forward()
         if k == 6:
-            normalize(4)
-            project_some(1, lambda i: i + 4)
-            cy.forward()
+            normalize(4, 2, 6)
+            project_last((32,))
+            tr[7].wait_recv()
+            tl[7].wait_recv()
+            normalize(4, 0, 2)
+            normalize(4, 6, 8)
+            project_last((0, 96))
             by.finish()
 
-    for slot in range(8):
-        rc(kv.at[slot], kv.at[8 + slot], KX + slot, xpeer[2]).wait_recv()
-
-    unit = 1.0 / math.sqrt(128)
+    kv_all = [rc(kv.at[d], kv.at[8 + d], KX + d, xpeer[2]) for d in range(8) if d != 4]
+    kv_all.extend(kv_last.values())
+    for c in kv_all:
+        c.wait_recv()
+
+    unit = math.log2(math.e) / math.sqrt(128)
 
     def attend(i, carry):
-        a, b = 4 + i, 3 - i
+        a, b = 4 + i, lax.rem(4 - i, 4)
         for h in range(2):
             hc = slice(h * 128, (h + 1) * 128)
             q = jnp.concatenate([qs[a, :, hc], qs[b, :, hc]], axis=0)
@@ -299,7 +342,7 @@
             vals = kv[:, :, h * 256 + 128:h * 256 + 256].reshape(2048, 128)
             sc = lax.dot_general(q, keys, (((1,), (1,)), ((), ())), preferred_element_type=F32)
             top = jnp.max(sc, axis=1, keepdims=True)
-            e = jnp.exp((sc - top) * unit)
+            e = jnp.exp2((sc - top) * unit)
             total = jnp.sum(e, axis=1, keepdims=True)
             o = jnp.dot(e.astype(BF), vals, preferred_element_type=F32) / total
             o = o.astype(BF)
@@ -307,7 +350,7 @@
             at[b, :, hc] = o[128:]
         rc(at.at[a], mx.at[8 - a], AZ + a, dev(lax.rem(z + 8 - a, 8), x, y, core)).start()
 
-        @pl.when(i < 3)
+        @pl.when(i > 0)
         def _():
             rc(at.at[b], mx.at[8 - b], AZ + b, dev(lax.rem(z + 8 - b, 8), x, y, core)).start()
 
@@ -325,7 +368,7 @@
     cy.finish()
     for c in od:
         c.wait_recv()
-    for n, pair in enumerate(((4, 3), (5, 2), (6, 1), (7, 0))):
+    for n, pair in enumerate(((4, 0), (5, 3), (6, 2), (7, 1))):
         for d in pair:
             if d > 0:
                 az[d].wait_recv()
@@ -355,8 +398,8 @@
         out_copy(q).wait()
     for c in sent:
         c.wait_send()
-    for slot in range(8):
-        rc(kv.at[slot], kv.at[8 + slot], KX + slot, xpeer[2]).wait_send()
+    for c in kv_all:
+        c.wait_send()
     for c in az.values():
         c.wait_send()
 
@@ -366,7 +409,6 @@
     freqs = jnp.exp(-math.log(10000.0) * jnp.arange(half_freq, dtype=F32) / half_freq)
     angles = timestep.astype(F32)[:, None] * freqs[None, :]
     embed = jnp.concatenate([jnp.cos(angles), jnp.sin(angles)], axis=1).astype(BF)
-    embed = jnp.broadcast_to(embed, (16, 2 * half_freq))
     anyspace = pl.BlockSpec(memory_space=pl.ANY)
     out = pl.pallas_call(
         kernel,

time: 104 us -> 103 us (level)
  Pallas kernels: 101 us -> 99.2 us
    pallas_call x1, Pallas kernels: 101 us -> 99.2 us  [on_device(): pl.pallas_call(kernel, out_shape=jax.ShapeDtypeStruct((128, 3072), BF), i...]
where the time goes in v3:
time: 103 us
  Pallas kernels  99.2 us (96%)
  local copies, waits for them, and re-layouts  2.06 us (2%)
    pallas_call x1, Pallas kernels, on_device(): pl.pallas_call(kernel, out_shape=jax.ShapeDtypeStruct((128, 3072), BF), i...  99.2 us
    unnamed x1, local copies, waits for them, and re-layouts  2.06 us

profile of v3, /device:TPU:1, one launch (start us, length us, event | category | flops | bytes accessed | tf_op | source)
XLA Modules:
  0.0 102.6 jit_solution(12970928297744376637)
XLA Ops:
  0.7 0.1 convert_bitcast_fusion
  0.7 0.6 pad_maximum_fusion.embed
  1.3 99.2 %sublayer.1 = bf16[128,3072]{1,0:T(8,128)(2,1)} custom-call(bf16[1,256]{1,0:T(2,128)(2,1)} %pad_maximum_fusion.embed, bf16[128,3072]{1,0:T(8,128)(2,1)} %bitcast.10, bf16[256,9216]{1,0:T(8,128)(2,1)} %wm_hbm.1, bf16[192,384]{1,0:T(8,128)(2,1)} %bitcast.11, bf16[8,3072]{1,0:T(8,128)(2,1)} %bitcast.12), custom_call_target="tpu_custom_call" | custom-call | tf_op jit(solution)/shard_map/sublayer/pallas_call | solution.py:413
  100.5 2.1 %copy.8 = bf16[1,128,3072]{2,1,0:T(8,128)(2,1)} copy(bf16[1,128,3072]{2,1,0:T(8,128)(2,1)} %bitcast.9) | data formatting | bytes 1572864

commit v4 on v3

--- a/solution.py
+++ b/solution.py
@@ -248,21 +248,25 @@
     }
 
     def project_last(starts):
-        acc = jnp.zeros((64, 768), F32)
         size = 64 // len(starts)
-        for a in range(2):
-            w = wq[a].reshape(1536, 768)
-            cut = slice(a * 1536, (a + 1) * 1536)
-            rows = jnp.concatenate([nrm[4, r:r + size, cut] for r in starts], axis=0)
-            acc += jnp.dot(rows, w, preferred_element_type=F32)
-        acc = acc.astype(BF)
+
+        def columns(*spans):
+            acc = jnp.zeros((64, 128 * len(spans)), F32)
+            for a in range(2):
+                cut = slice(a * 1536, (a + 1) * 1536)
+                w = jnp.concatenate(
+                    [wq[a, :, :, :, c:c + 128].reshape(1536, 128) for c in spans], axis=1)
+                rows = jnp.concatenate([nrm[4, r:r + size, cut] for r in starts], axis=0)
+                acc += jnp.dot(rows, w, preferred_element_type=F32)
+            return acc.astype(BF)
+
+        pairs = columns(128, 256, 512, 640)
         for n, r in enumerate(starts):
-            one = acc[n * size:(n + 1) * size]
-            qs[4, r:r + size, 0:128] = one[:, 0:128]
-            qs[4, r:r + size, 128:256] = one[:, 384:512]
-            kv[4, r:r + size, 0:256] = one[:, 128:384]
-            kv[4, r:r + size, 256:512] = one[:, 512:768]
+            kv[4, r:r + size, :] = pairs[n * size:(n + 1) * size]
             kv_last[r].start()
+        asks = columns(0, 384)
+        for n, r in enumerate(starts):
+            qs[4, r:r + size, :] = asks[n * size:(n + 1) * size]
 
     def project_some(count, slot_of):
         def body(i, carry):

time: 103 us -> 103 us (level)
  no operation moved by 1% of the time
where the time goes in v4:
time: 103 us
  Pallas kernels  99.2 us (96%)
  local copies, waits for them, and re-layouts  2.06 us (2%)
    pallas_call x1, Pallas kernels, on_device(): pl.pallas_call(kernel, out_shape=jax.ShapeDtypeStruct((128, 3072), BF), i...  99.2 us
    unnamed x1, local copies, waits for them, and re-layouts  2.06 us

profile of v4, /device:TPU:1, one launch (start us, length us, event | category | flops | bytes accessed | tf_op | source)
XLA Modules:
  0.0 102.6 jit_solution(1168199325725124408)
XLA Ops:
  0.7 0.1 convert_bitcast_fusion
  0.7 0.6 pad_maximum_fusion.embed
  1.3 99.2 %sublayer.1 = bf16[128,3072]{1,0:T(8,128)(2,1)} custom-call(bf16[1,256]{1,0:T(2,128)(2,1)} %pad_maximum_fusion.embed, bf16[128,3072]{1,0:T(8,128)(2,1)} %bitcast.10, bf16[256,9216]{1,0:T(8,128)(2,1)} %wm_hbm.1, bf16[192,384]{1,0:T(8,128)(2,1)} %bitcast.11, bf16[8,3072]{1,0:T(8,128)(2,1)} %bitcast.12), custom_call_target="tpu_custom_call" | custom-call | tf_op jit(solution)/shard_map/sublayer/pallas_call | solution.py:417
  100.5 2.1 %copy.8 = bf16[1,128,3072]{2,1,0:T(8,128)(2,1)} copy(bf16[1,128,3072]{2,1,0:T(8,128)(2,1)} %bitcast.9) | data formatting | bytes 1572864
